TPU v7x, 32 devices: a whole 2x2x4 slice. The times are simulated.
32 devices in a mesh: dp: 8 (over y, x, core), seq: 4 (over z).
Axes of the slice: x: 2, y: 2, z: 4, core: 2. Of those that a mesh axis runs over, the one named last changes fastest.
Arguments:
- tile_tokens: bfloat16 [8, 128, 3200], P('dp', 'seq'), may hold values from -6 to 6
- proj_weight: bfloat16 [3200, 8192], P('dp', 'seq')
- text_hidden: bfloat16 [8, 512, 8192], P('dp', 'seq'), may hold values from -6 to 6
- cotangent: bfloat16 [8, 512, 8192], P('dp', 'seq'), may hold values from -1.1953125 to 1.1953125
- norm_gain: float32 [8192], replicated, may hold values from 0.25 to 1.75
- placeholders: int32 [8, 128], P('dp'), may hold values from 0 to 511, as said below
- bucket_levels: int32 [8, 4, 3200], P('dp', 'seq'), may hold values from 2 to 16
- row_draws: float32 [8, 4, 3200], P('dp', 'seq'), may hold values from 0 to 1
- column_draws: float32 [8, 8192], P('dp', 'seq'), may hold values from 0 to 1
Outputs:
- weight_grad: float32 [3200, 8192], P('dp', 'seq')
- gain_grad: float32 [8192], replicated
Inputs may be any that keep to these rules, and one draw needn't show every extreme that they name: Each row is strictly increasing. Among the positions of one device's block of 128 positions stand at most 48 placeholders, and in every row some block holds exactly 48.
All inputs are finite; a program needn't handle non-finite values.
Results may differ from a plain program's by a relative error of at most 0.014.
Values may be sent and summed in bfloat16 or wider, within the bound.
No kernel may reach another device: no remote copies, remote signals or barrier semaphores. Data moves between devices by JAX's collectives and lax.ppermute only.
A program may use at most 64 MiB of HBM per device.

v0:
```python
import jax
import jax.numpy as jnp
from jax import lax
from jax.sharding import PartitionSpec as P

IMG_MOST = 48
EPSILON = 1e-06


def quantize(gradient, levels_now, rows_now, columns_now):
    bucket_norm = jnp.sqrt(jnp.sum(gradient * gradient, axis=1, keepdims=True) + EPSILON)
    step_count = levels_now.astype(jnp.float32)[:, None]
    offset = 0.25 + 0.25 * (rows_now[:, None] + columns_now[None, :])
    ratio = jnp.abs(gradient) / bucket_norm * step_count
    lower = jnp.floor(ratio)
    quantum = lower + jnp.clip(2.0 * (ratio - lower - offset) + 0.5, 0.0, 1.0)
    return jnp.sign(gradient) * bucket_norm * quantum / step_count


def on_device(
    tile_tokens,
    proj_weight,
    text_hidden,
    cotangent,
    norm_gain,
    placeholders,
    bucket_levels,
    row_draws,
    column_draws,
):
    seq_count = lax.axis_size("seq")
    seq_index = lax.axis_index("seq")
    replicas = lax.axis_size("dp")
    places = placeholders[0]
    image_total = places.shape[0]
    tok_rows = text_hidden.shape[1]
    model_width = text_hidden.shape[2]
    columns = proj_weight.shape[1]
    all_positions = tok_rows * seq_count
    zero_half = jnp.zeros((), jnp.bfloat16)
    own_text = text_hidden[0]
    own_cot = cotangent[0]
    gathered = lax.all_gather(tile_tokens[0], "seq", axis=0, tiled=True)
    patch_block = gathered
    embedded = jnp.dot(
        patch_block,
        lax.all_gather(proj_weight, "dp", axis=0, tiled=True),
        preferred_element_type=jnp.float32,
    ).astype(jnp.bfloat16)
    image_marks = jnp.zeros((all_positions,), jnp.int32).at[places].set(1)
    local_marks = lax.dynamic_slice_in_dim(image_marks, seq_index * tok_rows, tok_rows)
    is_image = local_marks[:, None] == 1
    owners = places // tok_rows
    owner_ids = jnp.arange(seq_count, dtype=jnp.int32)
    counts = jnp.sum((owners[:, None] == owner_ids[None, :]).astype(jnp.int32), axis=0)
    starts = jnp.cumsum(counts) - counts
    own_start = starts[seq_index]
    own_count = counts[seq_index]
    slot_ids = jnp.arange(IMG_MOST, dtype=jnp.int32)
    source_rows = jnp.clip(own_start + slot_ids, 0, image_total - 1)
    local_slots = jnp.clip(jnp.take(places, source_rows) - seq_index * tok_rows, 0, tok_rows - 1)
    slot_live = (slot_ids < own_count)[:, None]
    flat_index = owners * IMG_MOST + (
        jnp.arange(image_total, dtype=jnp.int32) - jnp.take(starts, owners)
    )
    outgoing = jnp.where(slot_live, jnp.take(own_cot, local_slots, axis=0), zero_half)
    returned = lax.all_to_all(outgoing[None], "seq", split_axis=2, concat_axis=0, tiled=True)
    image_cot = jnp.take(returned.reshape(-1, columns), flat_index, axis=0).astype(jnp.float32)
    emb_float = embedded.astype(jnp.float32)
    column_gain = lax.dynamic_slice_in_dim(norm_gain, seq_index * columns, columns)
    grad_in = image_cot * column_gain[None, :]
    squares, mixed = lax.psum(
        (jnp.sum(emb_float * emb_float, axis=1), jnp.sum(grad_in * emb_float, axis=1)), "seq"
    )
    inverse = lax.rsqrt(squares / model_width + EPSILON)[:, None]
    normed = emb_float * inverse
    emb_grad = ((grad_in - normed * (mixed[:, None] * inverse / model_width)) * inverse).astype(
        jnp.bfloat16
    )
    image_part = jnp.sum(image_cot * normed, axis=0)
    text_float = own_text.astype(jnp.float32)
    text_inverse = lax.rsqrt(jnp.mean(text_float * text_float, axis=1, keepdims=True) + EPSILON)
    text_terms = own_cot.astype(jnp.float32) * text_float * text_inverse
    text_part = jnp.sum(jnp.where(is_image, 0.0, text_terms), axis=0)
    placed_part = lax.dynamic_update_slice_in_dim(
        jnp.zeros((model_width,), jnp.float32), image_part, seq_index * columns, 0
    )
    gain_part = text_part + placed_part
    own_levels = bucket_levels[0, 0]
    own_row_draws = row_draws[0, 0]
    own_column_draws = column_draws[0]
    patch_block = gathered
    gradient = lax.dot_general(
        patch_block, emb_grad, (((0,), (0,)), ((), ())), preferred_element_type=jnp.float32
    )
    summed = lax.psum_scatter(
        quantize(gradient, own_levels, own_row_draws, own_column_draws).astype(jnp.bfloat16),
        "dp",
        scatter_dimension=0,
        tiled=True,
    ).astype(jnp.float32)
    gain_total = lax.psum(gain_part, ("dp", "seq"))
    return (summed / replicas, gain_total / replicas)


def solution(mesh):
    return jax.shard_map(
        on_device,
        mesh=mesh,
        in_specs=(
            P("dp", "seq", None),
            P("dp", "seq"),
            P("dp", "seq", None),
            P("dp", "seq", None),
            P(),
            P("dp", None),
            P("dp", "seq", None),
            P("dp", "seq", None),
            P("dp", "seq"),
        ),
        out_specs=(P("dp", "seq"), P()),
        check_vma=False,
    )
```

profile of v0, /device:TPU:0, one launch (start us, length us, event | category | flops | bytes accessed | tf_op | source)
XLA Modules:
  0.0 315.0 jit_solution(2458585537406789046)
XLA Ops:
  7.2 0.0 copy-start
  7.2 0.0 copy-start.6
  7.2 0.0 copy-start.5
  7.2 0.0 copy-start.4
  7.2 0.0 all-gather.3.cloned.1.call-start
  7.3 0.7 all-gather.3.cloned.1.call-update
  7.9 0.7 and_select_fusion.5
  8.6 0.1 convert_reduce_fusion.1
  8.7 0.2 reduce-window.9
  8.9 0.6 dynamic_slice.12
  9.5 0.7 fusion.34
  10.2 0.7 fusion.33
  10.9 1.4 gather_fusion
  12.3 0.7 fusion.31
  13.0 3.6 %gather_fusion.1 = bf16[48,8192]{1,0:T(8,128)(2,1)S(1)} fusion(bf16[128,8192]{1,0:T(8,128)(2,1)} %bitcast.74, s32[1024]{0:T(1024)S(1)} %pad_clamp_fusion.1), kind=kCustom, calls=%fused_computation.1 | custom fusion | bytes 1573056 | tf_op jit(solution)/shard_map/jit(_take)/gather | solution.py:66
  16.6 1.3 compare_and_fusion
  17.9 0.2 fusion.21
  18.1 6.8 %copy.22 = bf16[1,48,8192]{1,0,2:T(2,128)(2,1)} copy(bf16[1,48,8192]{2,1,0:T(8,128)(2,1)S(1)} %fusion.21) | data formatting | bytes 1572864 | tf_op jit(solution)/shard_map/jit(_where)/select_n | solution.py:66
  24.8 0.5 broadcast.575
  25.3 45.2 %reduce.4 = bf16[8192,48]{1,0:T(8,128)(2,1)S(1)} reduce(bf16[8192,1,48]{2,1,0:T(2,128)(2,1)} %bitcast.76, bf16[]{:T(256)} %broadcast.575), dimensions={1}, to_apply=%bitcast.63.reduce_sub_computation | reduce | bytes 1572866
  70.6 4.0 %reshape.423 = bf16[4,2,49152]{2,1,0:T(2,128)(2,1)} reshape(bf16[8192,48]{1,0:T(8,128)(2,1)S(1)} %reduce.4) | data formatting | bytes 1572864
  74.6 6.3 %all-to-all-start = ((bf16[4,2,49152]{2,1,0:T(2,128)(2,1)}), bf16[4,2,49152]{2,1,0:T(2,128)(2,1)S(1)}, u32[]{:S(2)}, u32[]{:S(2)}) async-start(bf16[4,2,49152]{2,1,0:T(2,128)(2,1)} %reshape.423), calls=%async_computation | async-start | bytes 1572864 | tf_op jit(solution)/shard_map/all_to_all | solution.py:67
  80.9 0.0 reduce-scatter.4.cloned.1.call-start
  80.9 0.7 dynamic_slice.14
  81.6 0.0 copy-done.6
  81.7 0.0 copy-done
  81.7 2.6 compare_and_fusion.1
  84.3 0.0 copy-done.5
  84.4 0.0 copy-done.4
  84.4 30.7 %all-gather = bf16[1,128,3200]{2,1,0:T(8,128)(2,1)S(1)} all-gather(bf16[1,32,3200]{2,1,0:T(8,128)(2,1)S(1)} %copy-done.4), channel_id=2, replica_groups=mesh['dp'=8,'seq'=4] {'seq'}, dimensions={1}, use_global_device_ids=true | all-gather | bytes 1024000 | tf_op jit(solution)/shard_map/all_gather | solution.py:43
  115.0 0.0 all-to-all-done
  115.0 4.6 %reshape.424 = bf16[8192,1,48]{2,1,0:T(2,128)(2,1)} reshape(bf16[4,2,49152]{2,1,0:T(2,128)(2,1)S(1)} %all-to-all-done) | data formatting | bytes 1572864
  119.6 8.1 %copy.23 = bf16[1,48,8192]{2,1,0:T(8,128)(2,1)S(1)} copy(bf16[1,48,8192]{1,0,2:T(2,128)(2,1)} %bitcast.77) | data formatting | bytes 1572864 | tf_op jit(solution)/shard_map/all_to_all | solution.py:67
  127.8 0.6 all_to_all.12
  128.4 0.4 copy.24
  128.8 0.9 gather_fusion.2
  129.7 0.0 copy-start.3
  129.8 0.0 all-gather.3.cloned.1.call-done
  129.8 7.1 %multiply_reduce_fusion.1 = (f32[128]{0:T(128)S(1)}, f32[128,2048]{1,0:T(8,128)S(1)}) fusion(bf16[3200,2048]{1,0:T(8,128)(2,1)} %all-gather.3.cloned.1.call-done, bf16[1,128,3200]{2,1,0:T(8,128)(2,1)S(1)} %all-gather), kind=kOutput, calls=%fused_computation.31 | convolution fusion | flops 1678770048 | bytes 14975488 | tf_op jit(solution)/shard_map/dot_general | solution.py:45
  136.8 0.0 copy-start.2
  136.9 11.1 %psum.21 = f32[128]{0:T(128)S(1)} all-reduce(f32[128]{0:T(128)S(1)} %get-tuple-element.22), channel_id=1, replica_groups=mesh['dp'=8,'seq'=4] {'seq'}, use_global_device_ids=true, to_apply=%region_3.4 | all-reduce | flops 128 | bytes 1024 | tf_op jit(solution)/shard_map/psum | solution.py:72
  148.0 0.4 fusion.17
  148.4 8.4 %psum.22 = f32[128]{0:T(128)S(1)} all-reduce(f32[128]{0:T(128)S(1)} %get-tuple-element.13), channel_id=1, replica_groups=mesh['dp'=8,'seq'=4] {'seq'}, use_global_device_ids=true, to_apply=%region_5.6 | all-reduce | flops 128 | bytes 1024 | tf_op jit(solution)/shard_map/psum | solution.py:72
  156.8 0.0 copy-done.3
  156.8 0.0 copy-done.2
  156.8 0.0 copy-start.7
  156.8 5.1 %multiply_reduce_fusion = (f32[3200]{0:T(1024)S(1)}, f32[2048,3200]{1,0:T(8,128)S(1)}) fusion(bf16[1,128,3200]{2,1,0:T(8,128)(2,1)S(1)} %all-gather, f32[128,2048]{1,0:T(8,128)} %copy-done.2, f32[128]{0:T(128)S(1)} %multiply_multiply_fusion, f32[128]{0:T(128)S(1)} %add_rsqrt_fusion.1, f32[2048]{0:T(1024)S(1)} %dynamic_slice.14, ...), kind=kOutput, calls=%fused_computation.12 | convolution fusion | flops 1692922752 | bytes 28628608 | tf_op jit(solution)/shard_map/dot_general | solution.py:93
  162.0 0.0 copy-done.7
  162.0 22.2 %fusion.6 = bf16[3200,2048]{0,1:T(8,128)(2,1)} fusion(f32[2048,3200]{1,0:T(8,128)S(1)} %get-tuple-element.25, f32[3200]{0:T(1024)S(1)} %convert_reduce_fusion, f32[2048]{0:T(1024)S(1)} %bitcast.79, f32[3200]{0:T(1024)S(1)} %reduce.2, f32[3200]{0:T(1024)S(1)} %add_sqrt_fusion), kind=kLoop, calls=%fused_computation.13 | loop fusion | flops 117964800 | bytes 39368192 | tf_op jit(solution)/shard_map/convert_element_type | solution.py:97
  184.1 18.3 %copy.26 = bf16[3200,2048]{1,0:T(8,128)(2,1)} copy(bf16[3200,2048]{0,1:T(8,128)(2,1)} %fusion.6) | data formatting | bytes 26214400
  202.5 0.0 copy-start.1
  202.5 0.0 reduce-scatter.4.cloned.1.call-update
  202.5 1.0 scatter_custom_fusion
  203.5 0.1 dynamic-slice_compare_fusion
  203.6 2.1 fusion.10
  205.7 0.0 copy-done.1
  205.7 2.6 fusion.9
  208.3 41.3 %psum.23 = f32[8192]{0:T(1024)S(1)} all-reduce(f32[8192]{0:T(1024)S(1)} %add_dynamic-update-slice_fusion), channel_id=1, replica_groups=mesh['dp'=8,'seq'=4] {'dp','seq'}, use_global_device_ids=true, to_apply=%region_12.13 | all-reduce | flops 8192 | bytes 65536 | tf_op jit(solution)/shard_map/psum | solution.py:102
  249.7 0.6 broadcast_multiply_fusion
  250.3 47.4 %reduce-scatter.4.cloned.1.call-done = bf16[400,2048]{1,0:T(8,128)(2,1)} async-done(((bf16[3200,2048]{1,0:T(8,128)(2,1)}), bf16[400,2048]{1,0:T(8,128)(2,1)}) %reduce-scatter.4.cloned.1.call-update) | async-done | bytes 1638416
  297.7 2.8 copy.27
  300.5 2.5 convert_multiply_fusion.2
  303.0 5.2 %copy.25 = f32[400,2048]{1,0:T(8,128)} copy(f32[400,2048]{0,1:T(8,128)} %convert_multiply_fusion.2) | data formatting | bytes 6553600
  (14 shorter events, 0.2 us)
Async XLA Ops:
  7.2 74.5 %copy-start = (s32[1,128]{1,0:T(1,128)S(1)}, s32[1,128]{1,0:T(1,128)}, u32[]{:S(2)}) copy-start(s32[1,128]{1,0:T(1,128)} %param.14) | copy-start | bytes 1540
  7.2 74.5 %copy-start.6 = (f32[1,1,3200]{2,1,0:T(1,128)S(1)}, f32[1,1,3200]{2,1,0:T(1,128)}, u32[]{:S(2)}) copy-start(f32[1,1,3200]{2,1,0:T(1,128)} %param.16) | copy-start | bytes 38404
  7.2 77.1 %copy-start.5 = (s32[1,1,3200]{2,1,0:T(1,128)S(1)}, s32[1,1,3200]{2,1,0:T(1,128)}, u32[]{:S(2)}) copy-start(s32[1,1,3200]{2,1,0:T(1,128)} %param.15) | copy-start | bytes 38404
  7.2 77.2 %copy-start.4 = (bf16[1,32,3200]{2,1,0:T(8,128)(2,1)S(1)}, bf16[1,32,3200]{2,1,0:T(8,128)(2,1)}, u32[]{:S(2)}) copy-start(bf16[1,32,3200]{2,1,0:T(8,128)(2,1)} %param.9) | copy-start | bytes 614404
  7.2 122.6 %all-gather.3.cloned.1.call-start = ((), (), s32[]{:S(2)}) async-start(), calls=%async_computation.2 | async-start | bytes 14745600 | tf_op jit(solution)/shard_map/all_gather | solution.py:47
  74.6 40.5 %all-to-all-start = ((bf16[4,2,49152]{2,1,0:T(2,128)(2,1)}), bf16[4,2,49152]{2,1,0:T(2,128)(2,1)S(1)}, u32[]{:S(2)}, u32[]{:S(2)}) async-start(bf16[4,2,49152]{2,1,0:T(2,128)(2,1)} %reshape.423), calls=%async_computation | async-start | bytes 1572864 | tf_op jit(solution)/shard_map/all_to_all | solution.py:67
  80.9 216.8 %reduce-scatter.4.cloned.1.call-start = ((), (), s32[]{:S(2)}) async-start(), calls=%async_computation.3 | async-start | bytes 14745600
  129.7 27.0 %copy-start.3 = (bf16[128,2048]{1,0:T(8,128)(2,1)}, bf16[128,2048]{1,0:T(8,128)(2,1)S(1)}, u32[]{:S(2)}) copy-start(bf16[128,2048]{1,0:T(8,128)(2,1)S(1)} %gather_fusion.2) | copy-start | bytes 1572868
  136.8 19.9 %copy-start.2 = (f32[128,2048]{1,0:T(8,128)}, f32[128,2048]{1,0:T(8,128)S(1)}, u32[]{:S(2)}) copy-start(f32[128,2048]{1,0:T(8,128)S(1)} %get-tuple-element.23) | copy-start | bytes 3145732
  156.8 5.2 %copy-start.7 = (f32[1,2048]{1,0:T(1,128)S(1)}, f32[1,2048]{1,0:T(1,128)}, u32[]{:S(2)}) copy-start(f32[1,2048]{1,0:T(1,128)} %param.17) | copy-start | bytes 24580
  202.5 3.2 %copy-start.1 = (bf16[1,128,8192]{2,1,0:T(8,128)(2,1)S(1)}, bf16[1,128,8192]{2,1,0:T(8,128)(2,1)}, u32[]{:S(2)}) copy-start(bf16[1,128,8192]{2,1,0:T(8,128)(2,1)} %param.12) | copy-start | bytes 6291460
Sparse Core Ops, SparseCore 0:
  9.9 76.9 all-gather.2
  202.6 95.0 reduce-scatter.3
where the time goes:
time: 316 us; the launch traced here: 315 us
  blocking collectives  91.5 us (29%)
  other arithmetic  82.2 us (26%)
  local copies, waits for them, and re-layouts  60.3 us (19%)
  waiting for transfers between devices  48.1 us (15%)
  between operations  14.3 us (5%)
  matrix products  12.2 us (4%)
  starting transfers between devices  6.39 us (2%)
    unnamed x3, waiting for transfers between devices  48.1 us
    unnamed x2, other arithmetic  45.3 us
    psum x1, blocking collectives, on_device(): gain_total = lax.psum(gain_part, ('dp', 'seq'))  41.3 us
    unnamed x22, local copies, waits for them, and re-layouts  35.4 us
    all_gather x1, blocking collectives, on_device(): gathered = lax.all_gather(tile_tokens[0], 'seq', axis=0, tiled=True)  30.7 us
    convert_element_type x1, other arithmetic, on_device(): quantize(gradient, own_levels, own_row_draws, own_column_draws)  22.2 us
    psum x2, blocking collectives, on_device(): lax.psum((jnp.sum(emb_float * emb_float, axis=1), jnp.sum(grad_in * emb_f...  19.5 us
    all_to_all x3, local copies, waits for them, and re-layouts, on_device(): lax.all_to_all(outgoing[None], 'seq', split_axis=2, concat_axis=0, tiled=...  9.14 us
  transfers between devices with their start and end apart: 3, of which 1 were waited for; matrix products, arithmetic and copies ran while one was open for 29% of the time, Pallas kernels for 0%

commit v1 on v0

--- a/solution.py
+++ b/solution.py
@@ -40,7 +40,12 @@
     zero_half = jnp.zeros((), jnp.bfloat16)
     own_text = text_hidden[0]
     own_cot = cotangent[0]
-    gathered = lax.all_gather(tile_tokens[0], "seq", axis=0, tiled=True)
+    ring = [tile_tokens[0]]
+    for hop in range(3):
+        ring.append(lax.ppermute(ring[-1], "seq", [(dev, (dev + 1) % 4) for dev in range(4)]))
+    gathered = jnp.roll(
+        jnp.concatenate(ring[::-1], axis=0), (lax.axis_index("seq") + 1) * ring[0].shape[0], axis=0
+    )
     patch_block = gathered
     embedded = jnp.dot(
         patch_block,

time: 316 us -> 340 us (1.076)
  blocking collectives: 91.5 us -> 57.5 us
  waiting for transfers between devices: 48.1 us -> 77.9 us
  local copies, waits for them, and re-layouts: 60.3 us -> 69.4 us
  matrix products: 12.2 us -> 20.7 us
  other arithmetic: 82.2 us -> 87.9 us
  starting transfers between devices: 6.39 us -> 10.4 us
    all_gather x1 -> x0, blocking collectives: 30.7 us -> none  [on_device(): gathered = lax.all_gather(tile_tokens[0], 'seq', axis=0, tiled=True)]
    ppermute x0 -> x3, waiting for transfers between devices: none -> 29.1 us  [on_device(): lax.ppermute(ring[-1], 'seq', [(dev, (dev + 1) % 4) for dev in range(4)])]
    dot_general x1, matrix products: 5.14 us -> 13.7 us  [on_device(): lax.dot_general(patch_block, emb_grad, (((0,), (0,)), ((), ())), preferre...]
    unnamed x22 -> x25, local copies, waits for them, and re-layouts: 35.4 us -> 41.4 us
    ppermute x0 -> x3, starting transfers between devices: none -> 3.94 us  [on_device(): lax.ppermute(ring[-1], 'seq', [(dev, (dev + 1) % 4) for dev in range(4)])]
  transfers between devices with their start and end apart: 3 -> 6, of which waited for: 1 -> 4; matrix products, arithmetic and copies ran while one was open for 29% -> 30% of each run, Pallas kernels for 0% -> 0%
where the time goes in v1:
time: 340 us; the launch traced here: 338 us
  other arithmetic  87.9 us (26%)
  waiting for transfers between devices  77.9 us (23%)
  local copies, waits for them, and re-layouts  69.4 us (20%)
  blocking collectives  57.5 us (17%)
  matrix products  20.7 us (6%)
  between operations  14.2 us (4%)
  starting transfers between devices  10.4 us (3%)
    unnamed x3, waiting for transfers between devices  48.8 us
    unnamed x2, other arithmetic  46.6 us
    unnamed x25, local copies, waits for them, and re-layouts  41.4 us
    psum x1, blocking collectives, on_device(): gain_total = lax.psum(gain_part, ('dp', 'seq'))  38.7 us
    ppermute x3, waiting for transfers between devices, on_device(): lax.ppermute(ring[-1], 'seq', [(dev, (dev + 1) % 4) for dev in range(4)])  29.1 us
    convert_element_type x1, other arithmetic, on_device(): quantize(gradient, own_levels, own_row_draws, own_column_draws)  24.2 us
    psum x2, blocking collectives, on_device(): lax.psum((jnp.sum(emb_float * emb_float, axis=1), jnp.sum(grad_in * emb_f...  18.8 us
    dot_general x1, matrix products, on_device(): lax.dot_general(patch_block, emb_grad, (((0,), (0,)), ((), ())), preferre...  13.7 us
  transfers between devices with their start and end apart: 6, of which 4 were waited for; matrix products, arithmetic and copies ran while one was open for 30% of the time, Pallas kernels for 0%

profile of v1, /device:TPU:0, one launch (start us, length us, event | category | flops | bytes accessed | tf_op | source)
XLA Modules:
  0.0 338.0 jit_solution(2211481303170452609)
XLA Ops:
  7.2 0.0 copy-start.1
  7.2 0.0 all-gather.2.cloned.1.call-start
  7.2 0.7 all-gather.2.cloned.1.call-update
  7.9 0.7 and_select_fusion.5
  8.6 0.1 convert_reduce_fusion.1
  8.7 0.2 reduce-window.9
  8.9 0.6 dynamic_slice.17
  9.5 0.7 fusion.36
  10.2 0.7 fusion.33
  10.8 1.4 gather_fusion
  12.3 0.7 fusion.31
  13.0 0.0 copy-done.1
  13.0 1.0 gather_fusion.1
  14.0 1.3 compare_and_fusion
  15.3 1.0 fusion.18
  16.3 8.9 %copy.22 = bf16[1,48,8192]{1,0,2:T(2,128)(2,1)} copy(bf16[1,48,8192]{2,1,0:T(8,128)(2,1)} %fusion.18) | data formatting | bytes 1572864 | tf_op jit(solution)/shard_map/jit(_where)/select_n | solution.py:71
  25.2 0.6 broadcast.573
  25.8 46.6 %reduce.3 = bf16[8192,48]{1,0:T(8,128)(2,1)} reduce(bf16[8192,1,48]{2,1,0:T(2,128)(2,1)} %bitcast.62, bf16[]{:T(256)} %broadcast.573), dimensions={1}, to_apply=%bitcast.53.reduce_sub_computation | reduce | bytes 1572866
  72.4 5.1 %reshape.422 = bf16[4,2,49152]{2,1,0:T(2,128)(2,1)} reshape(bf16[8192,48]{1,0:T(8,128)(2,1)} %reduce.3) | data formatting | bytes 1572864
  77.5 6.4 %all-to-all-start = ((bf16[4,2,49152]{2,1,0:T(2,128)(2,1)}), bf16[4,2,49152]{2,1,0:T(2,128)(2,1)S(1)}, u32[]{:S(2)}, u32[]{:S(2)}) async-start(bf16[4,2,49152]{2,1,0:T(2,128)(2,1)} %reshape.422), calls=%async_computation | async-start | bytes 1572864 | tf_op jit(solution)/shard_map/all_to_all | solution.py:72
  83.9 0.0 reduce-scatter.4.cloned.1.call-start
  83.9 0.0 copy-done.2
  83.9 2.0 collective-permute-start
  85.9 0.7 dynamic_slice.19
  86.6 0.0 copy-done.4
  86.7 2.6 compare_and_fusion.1
  89.3 16.0 %collective-permute-done = bf16[32,3200]{1,0:T(8,128)(2,1)S(1)} collective-permute-done((bf16[32,3200]{1,0:T(8,128)(2,1)S(1)}, bf16[32,3200]{1,0:T(8,128)(2,1)S(1)}, u32[]{:S(2)}, u32[]{:S(2)}) %collective-permute-start) | collective-permute-done | bytes 204832 | tf_op jit(solution)/shard_map/ppermute | solution.py:45
  105.3 1.9 collective-permute-start.1
  107.1 5.7 %collective-permute-done.1 = bf16[32,3200]{1,0:T(8,128)(2,1)S(1)} collective-permute-done((bf16[32,3200]{1,0:T(8,128)(2,1)S(1)}, bf16[32,3200]{1,0:T(8,128)(2,1)S(1)}, u32[]{:S(2)}, u32[]{:S(2)}) %collective-permute-start.1) | collective-permute-done | bytes 204832 | tf_op jit(solution)/shard_map/ppermute | solution.py:45
  112.8 0.1 collective-permute-start.2
  112.9 0.0 copy-done.3
  112.9 7.4 %collective-permute-done.2 = bf16[32,3200]{1,0:T(8,128)(2,1)S(1)} collective-permute-done((bf16[32,3200]{1,0:T(8,128)(2,1)S(1)}, bf16[32,3200]{1,0:T(8,128)(2,1)S(1)}, u32[]{:S(2)}, u32[]{:S(2)}) %collective-permute-start.2) | collective-permute-done | bytes 204832 | tf_op jit(solution)/shard_map/ppermute | solution.py:45
  120.4 0.7 constant_dynamic-update-slice_fusion.7
  121.1 0.7 constant_dynamic-update-slice_fusion.6
  121.8 0.7 constant_dynamic-update-slice_fusion.5
  122.5 0.7 constant_dynamic-update-slice_fusion.4
  123.2 0.7 constant_dynamic-update-slice_fusion.3
  123.8 0.7 constant_dynamic-update-slice_fusion.2
  124.5 0.7 constant_dynamic-update-slice_fusion.1
  125.2 0.7 constant_dynamic-update-slice_fusion
  125.9 0.0 all-to-all-done
  125.9 4.6 %reshape.423 = bf16[8192,1,48]{2,1,0:T(2,128)(2,1)} reshape(bf16[4,2,49152]{2,1,0:T(2,128)(2,1)S(1)} %all-to-all-done) | data formatting | bytes 1572864
  130.5 8.1 %copy.23 = bf16[1,48,8192]{2,1,0:T(8,128)(2,1)S(1)} copy(bf16[1,48,8192]{1,0,2:T(2,128)(2,1)} %bitcast.63) | data formatting | bytes 1572864 | tf_op jit(solution)/shard_map/all_to_all | solution.py:72
  138.7 1.5 all_to_all.12
  140.2 1.6 copy.24
  141.8 1.7 gather_fusion.2
  143.5 7.0 %multiply_reduce_fusion.1 = (f32[128]{0:T(128)S(1)}, f32[128,2048]{1,0:T(8,128)S(1)}) fusion(bf16[3200,2048]{1,0:T(8,128)(2,1)} %all-gather.2.cloned.1.call-done, bf16[256,3200]{1,0:T(8,128)(2,1)} %constant_dynamic-update-slice_fusion, s32[]{:T(128)S(6)} %select_n.196), kind=kOutput, calls=%fused_computation.31 | convolution fusion | flops 1678770048 | bytes 14975492 | tf_op jit(solution)/shard_map/dot_general | solution.py:50
  150.5 8.4 %psum.21 = f32[128]{0:T(128)S(1)} all-reduce(f32[128]{0:T(128)S(1)} %get-tuple-element.22), channel_id=1, replica_groups=mesh['dp'=8,'seq'=4] {'seq'}, use_global_device_ids=true, to_apply=%region_3.4 | all-reduce | flops 128 | bytes 1024 | tf_op jit(solution)/shard_map/psum | solution.py:77
  158.9 1.5 fusion.17
  160.4 10.3 %psum.22 = f32[128]{0:T(128)S(1)} all-reduce(f32[128]{0:T(128)S(1)} %get-tuple-element.13), channel_id=1, replica_groups=mesh['dp'=8,'seq'=4] {'seq'}, use_global_device_ids=true, to_apply=%region_5.6 | all-reduce | flops 128 | bytes 1024 | tf_op jit(solution)/shard_map/psum | solution.py:77
  170.7 13.7 %multiply_reduce_fusion = (f32[3200]{0:T(1024)S(1)}, f32[3200,2048]{0,1:T(8,128)}) fusion(f32[128,2048]{1,0:T(8,128)S(1)} %get-tuple-element.23, f32[128]{0:T(128)S(1)} %multiply_multiply_fusion, f32[128]{0:T(128)S(1)} %add_rsqrt_fusion.1, f32[2048]{0:T(1024)S(1)} %dynamic_slice.19, bf16[128,2048]{1,0:T(8,128)(2,1)} %gather_fusion.2, ...), kind=kOutput, calls=%fused_computation.12 | convolution fusion | flops 1692922752 | bytes 28628612 | tf_op jit(solution)/shard_map/dot_general | solution.py:98
  184.5 24.2 %fusion.6 = bf16[3200,2048]{0,1:T(8,128)(2,1)} fusion(f32[3200,2048]{0,1:T(8,128)} %get-tuple-element.25, f32[2048]{0:T(1024)S(1)} %bitcast.66, f32[3200]{0:T(1024)S(1)} %reduce.1, f32[3200]{0:T(1024)S(1)} %convert_reduce_fusion, f32[3200]{0:T(1024)S(1)} %add_sqrt_fusion), kind=kLoop, calls=%fused_computation.13 | loop fusion | flops 117964800 | bytes 39368192 | tf_op jit(solution)/shard_map/convert_element_type | solution.py:102
  208.6 18.3 %copy.26 = bf16[3200,2048]{1,0:T(8,128)(2,1)} copy(bf16[3200,2048]{0,1:T(8,128)(2,1)} %fusion.6) | data formatting | bytes 26214400
  227.0 0.0 reduce-scatter.4.cloned.1.call-update
  227.0 1.0 scatter_custom_fusion
  228.0 0.1 dynamic-slice_compare_fusion
  228.1 2.1 fusion.10
  230.2 3.1 fusion.9
  233.2 38.7 %psum.23 = f32[8192]{0:T(1024)S(1)} all-reduce(f32[8192]{0:T(1024)S(1)} %add_dynamic-update-slice_fusion), channel_id=1, replica_groups=mesh['dp'=8,'seq'=4] {'dp','seq'}, use_global_device_ids=true, to_apply=%region_12.13 | all-reduce | flops 8192 | bytes 65536 | tf_op jit(solution)/shard_map/psum | solution.py:107
  272.0 0.6 broadcast_multiply_fusion
  272.6 48.1 %reduce-scatter.4.cloned.1.call-done = bf16[400,2048]{1,0:T(8,128)(2,1)} async-done(((bf16[3200,2048]{1,0:T(8,128)(2,1)}), bf16[400,2048]{1,0:T(8,128)(2,1)}) %reduce-scatter.4.cloned.1.call-update) | async-done | bytes 1638416
  320.7 2.8 copy.27
  323.5 2.5 convert_multiply_fusion.2
  326.0 5.2 %copy.25 = f32[400,2048]{1,0:T(8,128)} copy(f32[400,2048]{0,1:T(8,128)} %convert_multiply_fusion.2) | data formatting | bytes 6553600
  (22 shorter events, 0.2 us)
Async XLA Ops:
  7.2 5.8 %copy-start.1 = (bf16[1,128,8192]{2,1,0:T(8,128)(2,1)S(1)}, bf16[1,128,8192]{2,1,0:T(8,128)(2,1)}, u32[]{:S(2)}) copy-start(bf16[1,128,8192]{2,1,0:T(8,128)(2,1)} %param.12) | copy-start | bytes 6291460
  7.2 136.3 %all-gather.2.cloned.1.call-start = ((), (), s32[]{:S(2)}) async-start(), calls=%async_computation.2 | async-start | bytes 14745600 | tf_op jit(solution)/shard_map/all_gather | solution.py:52
  25.8 58.1 %copy-start.2 = (bf16[1,32,3200]{2,1,0:T(8,128)(2,1)S(1)}, bf16[1,32,3200]{2,1,0:T(8,128)(2,1)}, u32[]{:S(2)}) copy-start(bf16[1,32,3200]{2,1,0:T(8,128)(2,1)} %param.9) | copy-start | bytes 614404
  25.8 60.8 %copy-start.4 = (f32[1,1,3200]{2,1,0:T(1,128)S(1)}, f32[1,1,3200]{2,1,0:T(1,128)}, u32[]{:S(2)}) copy-start(f32[1,1,3200]{2,1,0:T(1,128)} %param.16) | copy-start | bytes 38404
  25.8 60.9 %copy-start = (s32[1,128]{1,0:T(1,128)S(1)}, s32[1,128]{1,0:T(1,128)}, u32[]{:S(2)}) copy-start(s32[1,128]{1,0:T(1,128)} %param.14) | copy-start | bytes 1540
  25.8 87.1 %copy-start.3 = (s32[1,1,3200]{2,1,0:T(1,128)S(1)}, s32[1,1,3200]{2,1,0:T(1,128)}, u32[]{:S(2)}) copy-start(s32[1,1,3200]{2,1,0:T(1,128)} %param.15) | copy-start | bytes 38404
  77.5 48.4 %all-to-all-start = ((bf16[4,2,49152]{2,1,0:T(2,128)(2,1)}), bf16[4,2,49152]{2,1,0:T(2,128)(2,1)S(1)}, u32[]{:S(2)}, u32[]{:S(2)}) async-start(bf16[4,2,49152]{2,1,0:T(2,128)(2,1)} %reshape.422), calls=%async_computation | async-start | bytes 1572864 | tf_op jit(solution)/shard_map/all_to_all | solution.py:72
  83.9 236.8 %reduce-scatter.4.cloned.1.call-start = ((), (), s32[]{:S(2)}) async-start(), calls=%async_computation.3 | async-start | bytes 14745600
  83.9 21.4 %collective-permute-start = (bf16[32,3200]{1,0:T(8,128)(2,1)S(1)}, bf16[32,3200]{1,0:T(8,128)(2,1)S(1)}, u32[]{:S(2)}, u32[]{:S(2)}) collective-permute-start(bf16[32,3200]{1,0:T(8,128)(2,1)S(1)} %bitcast.65), channel_id=1, source_target_pairs={{0,1},{1,2},{2,3},{3,0},{4,5},{5,6},{6,7},{7,4},{8,9},{9,10},{10,1... | collective-permute-start | bytes 614408 | tf_op jit(solution)/shard_map/ppermute | solution.py:45
  105.3 7.6 %collective-permute-start.1 = (bf16[32,3200]{1,0:T(8,128)(2,1)S(1)}, bf16[32,3200]{1,0:T(8,128)(2,1)S(1)}, u32[]{:S(2)}, u32[]{:S(2)}) collective-permute-start(bf16[32,3200]{1,0:T(8,128)(2,1)S(1)} %collective-permute-done), channel_id=1, source_target_pairs={{0,1},{1,2},{2,3},{3,0},{4,5},{5,6},{6,7},{7,4},{8,9},{9,10},{10,1... | collective-permute-start | bytes 614408 | tf_op jit(solution)/shard_map/ppermute | solution.py:45
  112.8 7.6 %collective-permute-start.2 = (bf16[32,3200]{1,0:T(8,128)(2,1)S(1)}, bf16[32,3200]{1,0:T(8,128)(2,1)S(1)}, u32[]{:S(2)}, u32[]{:S(2)}) collective-permute-start(bf16[32,3200]{1,0:T(8,128)(2,1)S(1)} %collective-permute-done.1), channel_id=1, source_target_pairs={{0,1},{1,2},{2,3},{3,0},{4,5},{5,6},{6,7},{7,4},{8,9},{9,10},{10,1... | collective-permute-start | bytes 614408 | tf_op jit(solution)/shard_map/ppermute | solution.py:45
  170.7 13.7 %copy-start.5 = (f32[1,2048]{1,0:T(1,128)S(1)}, f32[1,2048]{1,0:T(1,128)}, u32[]{:S(2)}) copy-start(f32[1,2048]{1,0:T(1,128)} %param.17) | copy-start | bytes 24580
Sparse Core Ops, SparseCore 0:
  9.9 76.9 all-gather.1
  227.1 93.5 reduce-scatter.3
